TPU v7x, 32 devices: a whole 2x2x4 slice. The times are simulated.
32 devices in a mesh: dp: 8 (over y, x, core), tensor: 4 (over z).
Axes of the slice: x: 2, y: 2, z: 4, core: 2. Of those that a mesh axis runs over, the one named last changes fastest.
Arguments:
- tokens: bfloat16 [128, 8192], P('dp'), may hold values from -6 to 6
- norm_gain: bfloat16 [8192], replicated, may hold values from 0.099609375 to 1.8984375
- w_query: bfloat16 [8192, 8192], P('dp', 'tensor'), may hold values from -0.0625 to 0.0625
- w_key: bfloat16 [8192, 1024], P('dp', 'tensor'), may hold values from -0.0625 to 0.0625
- w_value: bfloat16 [8192, 1024], P('dp', 'tensor'), may hold values from -0.0625 to 0.0625
- check_column: bfloat16 [8192], replicated, may hold values from -6 to 6
- key_cache: bfloat16 [4096, 16, 8, 128], P('dp', None, 'tensor'), may hold values from -320 to 320
- value_cache: bfloat16 [4096, 16, 8, 128], P('dp', None, 'tensor'), may hold values from -6 to 6
- page_table: int32 [128, 32], P('dp'), may hold values from 0 to 511, as said below
- lengths: int32 [128], P('dp'), may hold values from 1 to 512, as said below
- tol_counts: int32 [128], replicated, may hold values from 0 to 7
Outputs:
- attention: bfloat16 [128, 8192], P('dp', 'tensor')
- excess: float32 [], replicated
Inputs may be any that keep to these rules, and one draw needn't show every extreme that they name: page_table holds pool pages of the index of dp that holds the sequence; the 16 sequences of one index of dp own distinct pages and together own all 512 of them. `lengths`: some sequence holds exactly 512 cached tokens.
All inputs are finite; a program needn't handle non-finite values.
Results may differ from a plain program's by a relative error of at most 0.007.
The roundings to bfloat16 on the way count: a program that leaves them out, or rounds other values in their place, can miss the bound.
Values may be sent and summed in bfloat16 or wider, within the bound.
A program may use at most 64 MiB of HBM per device.

v0:
```python
import functools
import math

import jax
import jax.numpy as jnp
from jax import lax
from jax.experimental import pallas as pl
from jax.experimental.pallas import tpu as pltpu
from jax.sharding import PartitionSpec as P

EPSILON = 1e-06
ROPE_BASE = 1000000.0
TOL_STEP = 0.25
MESH = pl.DeviceIdType.MESH
F32 = jnp.float32
BF16 = jnp.bfloat16
UNROLL = 4
LANES = 128


def step_kernel(
    dp,
    tp,
    table_ref,
    lengths_ref,
    counts_ref,
    tokens_ref,
    gain_ref,
    check_ref,
    wq_hbm,
    wk_hbm,
    wv_hbm,
    keys_hbm,
    values_hbm,
    out_ref,
    excess_ref,
    weights,
    keys,
    values,
    outgoing,
    spread,
    parts,
    from_pair,
    from_chips,
    queries,
    new_keys,
    new_values,
    mixed,
    sums_all,
    sums_own,
    shares,
    excess_all,
    excess_own,
    load_sems,
    a2a_send,
    a2a_recv,
    pair_send,
    pair_recv,
    chip_send,
    chip_recv,
    sum_send,
    sum_recv,
    exc_send,
    exc_recv,
):
    chips = dp // 2
    me = lax.axis_index("dp")
    zed = lax.axis_index("tensor")
    chip, core = me // 2, me % 2
    seqs, width = tokens_ref.shape
    depth = width // dp
    q_width, kv_width = wq_hbm.shape[1], wk_hbm.shape[1]
    total = q_width + 2 * kv_width
    chunks, _, _, chunk = parts.shape
    head = keys_hbm.shape[2]
    q_heads, kv_heads = q_width // head, kv_width // head
    group = q_heads // kv_heads
    pages = table_ref.shape[1]
    page_rows = keys_hbm.shape[1]

    barrier = pltpu.get_barrier_semaphore()
    for k in range(1, dp):
        pl.semaphore_signal(
            barrier, inc=1, device_id=((me + k) % dp, zed), device_id_type=MESH
        )
    for k in range(1, tp):
        pl.semaphore_signal(
            barrier, inc=1, device_id=(me, (zed + k) % tp), device_id_type=MESH
        )

    loads = [
        pltpu.make_async_copy(wq_hbm, weights.at[:, pl.ds(0, q_width)], load_sems.at[0]),
        pltpu.make_async_copy(wk_hbm, weights.at[:, pl.ds(q_width, kv_width)], load_sems.at[1]),
        pltpu.make_async_copy(
            wv_hbm, weights.at[:, pl.ds(q_width + kv_width, kv_width)], load_sems.at[2]
        ),
        pltpu.make_async_copy(keys_hbm, keys, load_sems.at[3]),
        pltpu.make_async_copy(values_hbm, values, load_sems.at[4]),
    ]
    for load in loads:
        load.start()

    square = jnp.zeros((seqs, LANES), F32)
    for j in range(width // LANES):
        part = tokens_ref[:, j * LANES : (j + 1) * LANES].astype(F32)
        square = square + part * part
    scale = lax.rsqrt(jnp.sum(square, axis=1, keepdims=True) / width + EPSILON)
    gains = gain_ref[...].astype(F32)
    for j in range(width // LANES):
        part = tokens_ref[:, j * LANES : (j + 1) * LANES].astype(F32)
        at = j * LANES % depth
        outgoing[j * LANES // depth, :, at : at + LANES] = (
            part * scale * gains[j : j + 1]
        ).astype(BF16)
    spread[0, 0] = outgoing[me]

    pl.semaphore_wait(barrier, dp - 1 + tp - 1)

    a2a = []
    for dc in range(chips - 1, -1, -1):
        for q in range(2):
            if dc == 0 and q == 0:
                continue
            target = ((chip + dc) % chips) * 2 + (core + q) % 2
            copy = pltpu.make_async_remote_copy(
                src_ref=outgoing.at[target],
                dst_ref=spread.at[q, dc],
                send_sem=a2a_send.at[q, dc],
                recv_sem=a2a_recv.at[q, dc],
                device_id=(target, zed),
                device_id_type=MESH,
            )
            copy.start()
            a2a.append(copy)

    checks = check_ref[...].astype(F32)
    checked = jnp.zeros((seqs, LANES), F32)
    for j in range(width // LANES):
        at = j * LANES % depth
        part = outgoing[j * LANES // depth, :, at : at + LANES].astype(F32)
        checked = checked + part * checks[j : j + 1]

    seq_row = lax.broadcasted_iota(jnp.int32, (seqs, LANES), 0)
    positions = jnp.zeros((seqs, LANES), F32)
    for s in range(seqs):
        positions = jnp.where(seq_row == s, lengths_ref[s].astype(F32), positions)
    lane = lax.broadcasted_iota(jnp.int32, (seqs, head), 1)
    step = (lane % (head // 2)).astype(F32)
    angles = positions * jnp.exp(step * (-2.0 * math.log(ROPE_BASE) / head))
    cosine = jnp.cos(angles)
    sine = jnp.where(lane < head // 2, -1.0, 1.0) * jnp.sin(angles)

    for load in loads[:3]:
        load.wait()
    for copy in a2a:
        copy.wait_recv()

    pair_copies, chip_copies = [], []
    half = chips * seqs

    def project(c):
        product = jnp.dot(
            spread[...].reshape(dp * seqs, depth),
            weights[:, pl.ds(c * chunk, chunk)],
            preferred_element_type=F32,
        )
        parts[c, 1] = product[half:]
        copy = pltpu.make_async_remote_copy(
            src_ref=parts.at[c, 1],
            dst_ref=from_pair.at[c],
            send_sem=pair_send.at[c],
            recv_sem=pair_recv.at[c],
            device_id=(chip * 2 + (core + 1) % 2, zed),
            device_id_type=MESH,
        )
        copy.start()
        pair_copies.append(copy)
        parts[c, 0] = product[:half]
        return sum(product[:, i : i + LANES] for i in range(0, chunk, LANES))

    def pass_on(c):
        pair_copies[c].wait_recv()
        for dc in range(chips - 1, 0, -1):
            rows = pl.ds(dc * seqs, seqs)
            parts[c, 0, rows] = parts[c, 0, rows] + from_pair[c, rows]
            copy = pltpu.make_async_remote_copy(
                src_ref=parts.at[c, 0, rows],
                dst_ref=from_chips.at[c, dc - 1],
                send_sem=chip_send.at[c, dc - 1],
                recv_sem=chip_recv.at[c, dc - 1],
                device_id=(((chip + chips - dc) % chips) * 2 + core, zed),
                device_id_type=MESH,
            )
            copy.start()
            chip_copies.append(copy)

    def exchange(own, everyone, place, targets, send_sems, recv_sems):
        everyone[place] = own[...]
        copies = []
        for k, target in enumerate(targets):
            copy = pltpu.make_async_remote_copy(
                src_ref=own,
                dst_ref=everyone.at[place],
                send_sem=send_sems.at[k],
                recv_sem=recv_sems.at[k],
                device_id=target,
                device_id_type=MESH,
            )
            copy.start()
            copies.append(copy)
        return copies

    row_sum = jnp.zeros((dp * seqs, LANES), F32)
    for c in range(chunks):
        row_sum = row_sum + project(c)
        if c >= 1:
            pass_on(c - 1)
    for q in range(2):
        for dc in range(chips):
            owner = ((chip + chips - dc) % chips) * 2 + (core + q) % 2
            at = (q * chips + dc) * seqs
            share = row_sum[at : at + seqs]
            if q == 0 and dc == 0:
                share = share - jnp.where(zed == 0, checked, 0.0)
            shares[owner] = share
    turned_sums = jnp.transpose(shares[...].reshape(dp * seqs, LANES))
    excess_own[...] = jnp.sum(turned_sums, axis=0, keepdims=True)
    exc_copies = exchange(
        excess_own, excess_all, me, [((me + k) % dp, zed) for k in range(1, dp)], exc_send, exc_recv
    )
    pass_on(chunks - 1)
    for copy in exc_copies:
        copy.wait_recv()
    group_sum = excess_all[0]
    for k in range(1, dp):
        group_sum = group_sum + excess_all[k]
    sums_own[...] = group_sum
    sum_copies = exchange(
        sums_own, sums_all, zed, [(me, (zed + k) % tp) for k in range(1, tp)], sum_send, sum_recv
    )

    def rotate(vector):
        return (
            (vector * cosine + pltpu.roll(vector, head // 2, 1) * sine)
            .astype(BF16)
            .astype(F32)
        )

    for c in range(chunks):
        for copy in chip_copies[c * (chips - 1) : (c + 1) * (chips - 1)]:
            copy.wait_recv()
        own = parts[c, 0, pl.ds(0, seqs)] + from_pair[c, pl.ds(0, seqs)]
        for dc in range(1, chips):
            own = own + from_chips[c, dc - 1]
        for i in range(chunk // head):
            block = own[:, i * head : (i + 1) * head]
            index = c * (chunk // head) + i
            if index < q_heads:
                queries[:, index, :] = rotate(block)
            elif index < q_heads + kv_heads:
                k = index - q_heads
                turned = rotate(block)
                for g in range(group):
                    new_keys[:, k * group + g, :] = turned
            else:
                k = index - q_heads - kv_heads
                rounded = block.astype(BF16).astype(F32)
                for g in range(group):
                    new_values[:, k * group + g, :] = rounded

    span = pages * page_rows
    column = lax.broadcasted_iota(jnp.int32, (q_heads, span), 1)
    row = lax.broadcasted_iota(jnp.int32, (q_heads, span), 0)
    place = jnp.where(column % kv_heads == row // group, column // kv_heads, span)
    score_scale = head ** (-0.5)
    for load in loads[3:]:
        load.wait()

    def one_sequence(s, carry):
        owned = [table_ref[s, p] for p in range(pages)]
        length = lengths_ref[s]
        query = queries[s]
        cached = jnp.concatenate([keys[page] for page in owned], axis=0)
        scores = (
            lax.dot_general(
                query.astype(BF16),
                cached,
                (((1,), (1,)), ((), ())),
                preferred_element_type=F32,
            )
            * score_scale
        )
        new_score = jnp.sum(query * new_keys[s], axis=1, keepdims=True) * score_scale
        masked = jnp.where(place < length, scores, -jnp.inf)
        peak = jnp.maximum(jnp.max(masked, axis=1, keepdims=True), new_score)
        soft = jnp.exp(masked - peak)
        new_weight = jnp.exp(new_score - peak)
        denominator = jnp.sum(soft, axis=1, keepdims=True) + new_weight
        stored = jnp.concatenate([values[page] for page in owned], axis=0)
        result = jnp.dot(soft.astype(BF16), stored, preferred_element_type=F32)
        result = result + new_weight.astype(BF16).astype(F32) * new_values[s]
        mixed[s] = result / denominator
        return carry

    lax.fori_loop(0, seqs, one_sequence, 0, unroll=UNROLL)

    for h in range(q_heads):
        out_ref[:, h * head : (h + 1) * head] = mixed[:, h, :].astype(BF16)

    for copy in sum_copies:
        copy.wait_recv()
    grand = sums_all[0]
    for k in range(1, tp):
        grand = grand + sums_all[k]
    residual = grand / math.sqrt(total * tp)
    over = jnp.maximum(jnp.abs(residual) - TOL_STEP * counts_ref[...].astype(F32), 0.0)
    excess_ref[...] = jnp.sum(over, axis=1, keepdims=True) / math.sqrt(seqs * dp)

    for copy in a2a + pair_copies + chip_copies + sum_copies + exc_copies:
        copy.wait_send()


def body(
    dp,
    tp,
    tokens,
    norm_gain,
    w_query,
    w_key,
    w_value,
    check_column,
    key_cache,
    value_cache,
    page_table,
    lengths,
    tol_counts,
):
    seqs, width = tokens.shape
    head = key_cache.shape[-1]
    q_width, kv_width = w_query.shape[1], w_key.shape[1]
    total = q_width + 2 * kv_width
    q_heads = q_width // head
    depth = width // dp
    chips = dp // 2
    chunks = 5 if total % (5 * head) == 0 else 1
    chunk = total // chunks
    flat_keys = key_cache.reshape(key_cache.shape[0], -1, head)
    flat_values = value_cache.reshape(value_cache.shape[0], -1, head)

    smem = pl.BlockSpec(memory_space=pltpu.SMEM)
    vmem = pl.BlockSpec(memory_space=pltpu.VMEM)
    hbm = pl.BlockSpec(memory_space=pltpu.HBM)
    dma = pltpu.SemaphoreType.DMA
    attention, excess = pl.pallas_call(
        functools.partial(step_kernel, dp, tp),
        out_shape=(
            jax.ShapeDtypeStruct((seqs, q_width), BF16),
            jax.ShapeDtypeStruct((1, 1), F32),
        ),
        in_specs=[smem] * 2 + [vmem] * 4 + [hbm] * 5,
        out_specs=(vmem, vmem),
        scratch_shapes=[
            pltpu.VMEM((depth, total), BF16),
            pltpu.VMEM(flat_keys.shape, BF16),
            pltpu.VMEM(flat_values.shape, BF16),
            pltpu.VMEM((dp, seqs, depth), BF16),
            pltpu.VMEM((2, chips, seqs, depth), BF16),
            pltpu.VMEM((chunks, 2, chips * seqs, chunk), F32),
            pltpu.VMEM((chunks, chips * seqs, chunk), F32),
            pltpu.VMEM((chunks, chips - 1, seqs, chunk), F32),
            pltpu.VMEM((seqs, q_heads, head), F32),
            pltpu.VMEM((seqs, q_heads, head), F32),
            pltpu.VMEM((seqs, q_heads, head), F32),
            pltpu.VMEM((seqs, q_heads, head), F32),
            pltpu.VMEM((tp, 1, dp * seqs), F32),
            pltpu.VMEM((1, dp * seqs), F32),
            pltpu.VMEM((dp, seqs, LANES), F32),
            pltpu.VMEM((dp, 1, dp * seqs), F32),
            pltpu.VMEM((1, dp * seqs), F32),
            dma((5,)),
            dma((2, chips)),
            dma((2, chips)),
            dma((chunks,)),
            dma((chunks,)),
            dma((chunks, chips - 1)),
            dma((chunks, chips - 1)),
            dma((tp,)),
            dma((tp,)),
            dma((dp,)),
            dma((dp,)),
        ],
        compiler_params=pltpu.CompilerParams(
            collective_id=0, has_side_effects=True, vmem_limit_bytes=60 * 1024 * 1024
        ),
    )(
        page_table,
        lengths,
        tol_counts.reshape(1, -1),
        tokens,
        norm_gain.reshape(-1, LANES),
        check_column.reshape(-1, LANES),
        w_query,
        w_key,
        w_value,
        flat_keys,
        flat_values,
    )
    return attention, excess[0, 0]


def solution(mesh):
    return jax.shard_map(
        functools.partial(body, mesh.shape["dp"], mesh.shape["tensor"]),
        mesh=mesh,
        in_specs=(
            P("dp", None),
            P(),
            P("dp", "tensor"),
            P("dp", "tensor"),
            P("dp", "tensor"),
            P(),
            P("dp", None, "tensor", None),
            P("dp", None, "tensor", None),
            P("dp", None),
            P("dp"),
            P(),
        ),
        out_specs=(P("dp", "tensor"), P()),
        check_vma=False,
    )
```

profile of v0, /device:TPU:0, one launch (start us, length us, event | category | flops | bytes accessed | tf_op | source)
XLA Modules:
  0.0 32.5 jit_solution(17507563269420474158)
XLA Ops:
  0.6 28.6 %shard_map.122 = (bf16[16,2048]{1,0:T(8,128)(2,1)}, f32[1,1]{1,0:T(1,128)}) custom-call(s32[16,32]{1,0:T(8,128)} %table_ref.1, s32[16]{0:T(128)} %lengths_ref.1, s32[1,128]{1,0:T(1,128)} %bitcast.10, bf16[16,8192]{1,0:T(8,128)(2,1)} %tokens_ref.1, bf16[64,128]{1,0:T(8,128)(2,1)} %bitcast.8, bf16[64,128]{1,0:T(8,128)(2,1)} %bitcast.9, ...), custom_call_target="tpu_custom_call" | custom-call | tf_op jit(solution)/shard_map/pallas_call | solution.py:354
  29.2 1.5 %copy.15 = bf16[16,2048]{1,0:T(8,128)(2,1)} copy(bf16[16,2048]{1,0:T(8,128)(2,1)} %get-tuple-element.8) | data formatting | bytes 131072
where the time goes:
time: 32.7 us; the launch traced here: 32.5 us
  Pallas kernels  28.6 us (87%)
  between operations  2.39 us (7%)
  local copies, waits for them, and re-layouts  1.47 us (4%)
    pallas_call x1, Pallas kernels, body(): pl.pallas_call(functools.partial(step_kernel, dp, tp), out_shape=(jax.Sha...  28.6 us
    unnamed x1, local copies, waits for them, and re-layouts  1.47 us

commit v1 on v0

--- a/solution.py
+++ b/solution.py
@@ -21,12 +21,12 @@
 def step_kernel(
     dp,
     tp,
-    table_ref,
-    lengths_ref,
-    counts_ref,
-    tokens_ref,
-    gain_ref,
-    check_ref,
+    table_hbm,
+    lengths_hbm,
+    counts_hbm,
+    tokens_hbm,
+    gain_hbm,
+    check_hbm,
     wq_hbm,
     wk_hbm,
     wv_hbm,
@@ -34,9 +34,16 @@
     values_hbm,
     out_ref,
     excess_ref,
+    table_ref,
+    lengths_ref,
+    counts_ref,
+    tokens_ref,
+    gain_ref,
+    check_ref,
     weights,
     keys,
     values,
+    key_columns,
     outgoing,
     spread,
     parts,
@@ -51,6 +58,7 @@
     shares,
     excess_all,
     excess_own,
+    small_sems,
     load_sems,
     a2a_send,
     a2a_recv,
@@ -78,28 +86,49 @@
     pages = table_ref.shape[1]
     page_rows = keys_hbm.shape[1]
 
+    def partner(dc):
+        other, bit = chip, 1
+        while bit <= dc:
+            if dc // bit % 2:
+                other = other + bit - 2 * bit * (chip // bit % 2)
+            bit *= 2
+        return other
+
     barrier = pltpu.get_barrier_semaphore()
     for k in range(1, dp):
         pl.semaphore_signal(
             barrier, inc=1, device_id=((me + k) % dp, zed), device_id_type=MESH
         )
-    for k in range(1, tp):
-        pl.semaphore_signal(
-            barrier, inc=1, device_id=(me, (zed + k) % tp), device_id_type=MESH
-        )
-
+
+    small_loads = [
+        pltpu.make_async_copy(source, target, small_sems.at[i])
+        for i, (source, target) in enumerate(
+            [
+                (tokens_hbm, tokens_ref),
+                (gain_hbm, gain_ref),
+                (lengths_hbm, lengths_ref),
+                (check_hbm, check_ref),
+                (table_hbm, table_ref),
+                (counts_hbm, counts_ref),
+            ]
+        )
+    ]
+    for load in small_loads:
+        load.start()
     loads = [
         pltpu.make_async_copy(wq_hbm, weights.at[:, pl.ds(0, q_width)], load_sems.at[0]),
-        pltpu.make_async_copy(wk_hbm, weights.at[:, pl.ds(q_width, kv_width)], load_sems.at[1]),
+        pltpu.make_async_copy(wk_hbm, weights.at[:, pl.ds(q_width, kv_width)], load_sems.at[0]),
         pltpu.make_async_copy(
-            wv_hbm, weights.at[:, pl.ds(q_width + kv_width, kv_width)], load_sems.at[2]
+            wv_hbm, weights.at[:, pl.ds(q_width + kv_width, kv_width)], load_sems.at[0]
         ),
-        pltpu.make_async_copy(keys_hbm, keys, load_sems.at[3]),
-        pltpu.make_async_copy(values_hbm, values, load_sems.at[4]),
+        pltpu.make_async_copy(keys_hbm, keys, load_sems.at[1]),
+        pltpu.make_async_copy(values_hbm, values, load_sems.at[2]),
     ]
     for load in loads:
         load.start()
 
+    for load in small_loads[:2]:
+        load.wait()
     square = jnp.zeros((seqs, LANES), F32)
     for j in range(width // LANES):
         part = tokens_ref[:, j * LANES : (j + 1) * LANES].astype(F32)
@@ -112,27 +141,37 @@
         outgoing[j * LANES // depth, :, at : at + LANES] = (
             part * scale * gains[j : j + 1]
         ).astype(BF16)
-    spread[0, 0] = outgoing[me]
-
-    pl.semaphore_wait(barrier, dp - 1 + tp - 1)
-
-    a2a = []
+    spread[0] = outgoing[me]
+
+    pl.semaphore_wait(barrier, dp - 1 + (zed + tp - 1) // tp)
+
+    def greet_plane(k):
+        @pl.when((zed + k >= 0) & (zed + k < tp))
+        def _():
+            pl.semaphore_signal(barrier, inc=1, device_id=(me, zed + k), device_id_type=MESH)
+
+
     for dc in range(chips - 1, -1, -1):
         for q in range(2):
             if dc == 0 and q == 0:
                 continue
-            target = ((chip + dc) % chips) * 2 + (core + q) % 2
+            target = partner(dc) * 2 + (core + q) % 2
             copy = pltpu.make_async_remote_copy(
                 src_ref=outgoing.at[target],
-                dst_ref=spread.at[q, dc],
-                send_sem=a2a_send.at[q, dc],
-                recv_sem=a2a_recv.at[q, dc],
+                dst_ref=spread.at[q * chips + dc],
+                send_sem=a2a_send,
+                recv_sem=a2a_recv,
                 device_id=(target, zed),
                 device_id_type=MESH,
             )
             copy.start()
-            a2a.append(copy)
-
+
+    greet_plane(1)
+    for k in range(1, tp):
+        greet_plane(-k)
+
+    for load in small_loads[2:]:
+        load.wait()
     checks = check_ref[...].astype(F32)
     checked = jnp.zeros((seqs, LANES), F32)
     for j in range(width // LANES):
@@ -150,12 +189,32 @@
     cosine = jnp.cos(angles)
     sine = jnp.where(lane < head // 2, -1.0, 1.0) * jnp.sin(angles)
 
-    for load in loads[:3]:
-        load.wait()
-    for copy in a2a:
-        copy.wait_recv()
-
-    pair_copies, chip_copies = [], []
+    near = (pages + 1) // 2
+    far = pages - near
+    span = near * page_rows
+    no_page = jnp.zeros((page_rows, head), BF16)
+
+    def side_by_side(pool, s):
+        left = [pool[table_ref[s, p]] for p in range(near)]
+        right = [pool[table_ref[s, p]] for p in range(near, pages)] + [no_page] * (near - far)
+        return jnp.concatenate(
+            [jnp.concatenate(left, axis=0), jnp.concatenate(right, axis=0)], axis=1
+        )
+
+    def turn_keys(s, carry):
+        key_columns[s] = jnp.transpose(side_by_side(keys, s))
+        return carry
+
+    loads[3].wait()
+    lax.fori_loop(0, seqs, turn_keys, 0, unroll=UNROLL)
+
+    def wait_bytes(ref, sem):
+        pltpu.make_async_copy(ref, ref, sem).wait()
+
+    wait_bytes(weights, load_sems.at[0])
+    wait_bytes(spread.at[pl.ds(1, dp - 1)], a2a_recv)
+
+    pair_copies = []
     half = chips * seqs
 
     def project(c):
@@ -168,7 +227,7 @@
         copy = pltpu.make_async_remote_copy(
             src_ref=parts.at[c, 1],
             dst_ref=from_pair.at[c],
-            send_sem=pair_send.at[c],
+            send_sem=pair_send,
             recv_sem=pair_recv.at[c],
             device_id=(chip * 2 + (core + 1) % 2, zed),
             device_id_type=MESH,
@@ -186,38 +245,35 @@
             copy = pltpu.make_async_remote_copy(
                 src_ref=parts.at[c, 0, rows],
                 dst_ref=from_chips.at[c, dc - 1],
-                send_sem=chip_send.at[c, dc - 1],
-                recv_sem=chip_recv.at[c, dc - 1],
-                device_id=(((chip + chips - dc) % chips) * 2 + core, zed),
+                send_sem=chip_send,
+                recv_sem=chip_recv.at[c],
+                device_id=(partner(dc) * 2 + core, zed),
                 device_id_type=MESH,
             )
             copy.start()
-            chip_copies.append(copy)
-
-    def exchange(own, everyone, place, targets, send_sems, recv_sems):
+
+    def exchange(own, everyone, place, targets, send_sem, recv_sem):
         everyone[place] = own[...]
-        copies = []
-        for k, target in enumerate(targets):
-            copy = pltpu.make_async_remote_copy(
+        for target in targets:
+            pltpu.make_async_remote_copy(
                 src_ref=own,
                 dst_ref=everyone.at[place],
-                send_sem=send_sems.at[k],
-                recv_sem=recv_sems.at[k],
+                send_sem=send_sem,
+                recv_sem=recv_sem,
                 device_id=target,
                 device_id_type=MESH,
-            )
-            copy.start()
-            copies.append(copy)
-        return copies
+            ).start()
 
     row_sum = jnp.zeros((dp * seqs, LANES), F32)
+    passed = 0
     for c in range(chunks):
         row_sum = row_sum + project(c)
-        if c >= 1:
-            pass_on(c - 1)
+        if c >= 3:
+            pass_on(passed)
+            passed += 1
     for q in range(2):
         for dc in range(chips):
-            owner = ((chip + chips - dc) % chips) * 2 + (core + q) % 2
+            owner = partner(dc) * 2 + (core + q) % 2
             at = (q * chips + dc) * seqs
             share = row_sum[at : at + seqs]
             if q == 0 and dc == 0:
@@ -225,17 +281,23 @@
             shares[owner] = share
     turned_sums = jnp.transpose(shares[...].reshape(dp * seqs, LANES))
     excess_own[...] = jnp.sum(turned_sums, axis=0, keepdims=True)
-    exc_copies = exchange(
+    exchange(
         excess_own, excess_all, me, [((me + k) % dp, zed) for k in range(1, dp)], exc_send, exc_recv
     )
-    pass_on(chunks - 1)
-    for copy in exc_copies:
-        copy.wait_recv()
+    while passed < chunks:
+        pass_on(passed)
+        passed += 1
+    wait_bytes(excess_all.at[pl.ds(1, dp - 1)], exc_recv)
     group_sum = excess_all[0]
     for k in range(1, dp):
         group_sum = group_sum + excess_all[k]
     sums_own[...] = group_sum
-    sum_copies = exchange(
+
+    @pl.when(zed < tp - 1)
+    def _():
+        pl.semaphore_wait(barrier, tp - 1 - zed)
+
+    exchange(
         sums_own, sums_all, zed, [(me, (zed + k) % tp) for k in range(1, tp)], sum_send, sum_recv
     )
 
@@ -247,8 +309,7 @@
         )
 
     for c in range(chunks):
-        for copy in chip_copies[c * (chips - 1) : (c + 1) * (chips - 1)]:
-            copy.wait_recv()
+        wait_bytes(from_chips.at[c], chip_recv.at[c])
         own = parts[c, 0, pl.ds(0, seqs)] + from_pair[c, pl.ds(0, seqs)]
         for dc in range(1, chips):
             own = own + from_chips[c, dc - 1]
@@ -268,47 +329,50 @@
                 for g in range(group):
                     new_values[:, k * group + g, :] = rounded
 
-    span = pages * page_rows
-    column = lax.broadcasted_iota(jnp.int32, (q_heads, span), 1)
-    row = lax.broadcasted_iota(jnp.int32, (q_heads, span), 0)
-    place = jnp.where(column % kv_heads == row // group, column // kv_heads, span)
+    column = lax.broadcasted_iota(jnp.int32, (2 * q_heads, span), 1)
+    row = lax.broadcasted_iota(jnp.int32, (2 * q_heads, span), 0)
+    place = jnp.where(
+        column % kv_heads == row % q_heads // group,
+        column // kv_heads + row // q_heads * (span // kv_heads),
+        pages * page_rows,
+    )
     score_scale = head ** (-0.5)
-    for load in loads[3:]:
-        load.wait()
-
-    def one_sequence(s, carry):
-        owned = [table_ref[s, p] for p in range(pages)]
-        length = lengths_ref[s]
+    no_query = jnp.zeros((q_heads, head), BF16)
+    loads[4].wait()
+
+    def one_sequence(s):
         query = queries[s]
-        cached = jnp.concatenate([keys[page] for page in owned], axis=0)
-        scores = (
-            lax.dot_general(
-                query.astype(BF16),
-                cached,
-                (((1,), (1,)), ((), ())),
-                preferred_element_type=F32,
-            )
-            * score_scale
-        )
+        narrow = query.astype(BF16)
+        paired = jnp.concatenate(
+            [
+                jnp.concatenate([narrow, no_query], axis=1),
+                jnp.concatenate([no_query, narrow], axis=1),
+            ],
+            axis=0,
+        )
+        scores = jnp.dot(paired, key_columns[s], preferred_element_type=F32) * score_scale
         new_score = jnp.sum(query * new_keys[s], axis=1, keepdims=True) * score_scale
-        masked = jnp.where(place < length, scores, -jnp.inf)
-        peak = jnp.maximum(jnp.max(masked, axis=1, keepdims=True), new_score)
-        soft = jnp.exp(masked - peak)
+        masked = jnp.where(place < lengths_ref[s], scores, -jnp.inf)
+        highest = jnp.max(masked, axis=1, keepdims=True)
+        peak = jnp.maximum(jnp.maximum(highest[:q_heads], highest[q_heads:]), new_score)
+        soft = jnp.exp(masked - jnp.concatenate([peak, peak], axis=0))
         new_weight = jnp.exp(new_score - peak)
-        denominator = jnp.sum(soft, axis=1, keepdims=True) + new_weight
-        stored = jnp.concatenate([values[page] for page in owned], axis=0)
-        result = jnp.dot(soft.astype(BF16), stored, preferred_element_type=F32)
+        sums = jnp.sum(soft, axis=1, keepdims=True)
+        denominator = sums[:q_heads] + sums[q_heads:] + new_weight
+        result = jnp.dot(
+            soft.astype(BF16), side_by_side(values, s), preferred_element_type=F32
+        )
+        result = result[:q_heads, :head] + result[q_heads:, head:]
         result = result + new_weight.astype(BF16).astype(F32) * new_values[s]
         mixed[s] = result / denominator
-        return carry
-
-    lax.fori_loop(0, seqs, one_sequence, 0, unroll=UNROLL)
+
+    for s in range(seqs):
+        one_sequence(s)
 
     for h in range(q_heads):
         out_ref[:, h * head : (h + 1) * head] = mixed[:, h, :].astype(BF16)
 
-    for copy in sum_copies:
-        copy.wait_recv()
+    wait_bytes(sums_all.at[pl.ds(1, tp - 1)], sum_recv)
     grand = sums_all[0]
     for k in range(1, tp):
         grand = grand + sums_all[k]
@@ -316,8 +380,11 @@
     over = jnp.maximum(jnp.abs(residual) - TOL_STEP * counts_ref[...].astype(F32), 0.0)
     excess_ref[...] = jnp.sum(over, axis=1, keepdims=True) / math.sqrt(seqs * dp)
 
-    for copy in a2a + pair_copies + chip_copies + sum_copies + exc_copies:
-        copy.wait_send()
+    wait_bytes(spread.at[pl.ds(1, dp - 1)], a2a_send)
+    wait_bytes(from_pair, pair_send)
+    wait_bytes(from_chips, chip_send)
+    wait_bytes(sums_all.at[pl.ds(1, tp - 1)], sum_send)
+    wait_bytes(excess_all.at[pl.ds(1, dp - 1)], exc_send)
 
 
 def body(
@@ -347,24 +414,30 @@
     flat_keys = key_cache.reshape(key_cache.shape[0], -1, head)
     flat_values = value_cache.reshape(value_cache.shape[0], -1, head)
 
-    smem = pl.BlockSpec(memory_space=pltpu.SMEM)
     vmem = pl.BlockSpec(memory_space=pltpu.VMEM)
     hbm = pl.BlockSpec(memory_space=pltpu.HBM)
     dma = pltpu.SemaphoreType.DMA
     attention, excess = pl.pallas_call(
         functools.partial(step_kernel, dp, tp),
         out_shape=(
-            jax.ShapeDtypeStruct((seqs, q_width), BF16),
-            jax.ShapeDtypeStruct((1, 1), F32),
+            pltpu.VMEM((seqs, q_width), BF16),
+            pltpu.VMEM((1, 1), F32),
         ),
-        in_specs=[smem] * 2 + [vmem] * 4 + [hbm] * 5,
+        in_specs=[hbm] * 11,
         out_specs=(vmem, vmem),
         scratch_shapes=[
+            pltpu.SMEM(page_table.shape, jnp.int32),
+            pltpu.SMEM(lengths.shape, jnp.int32),
+            pltpu.VMEM((1, tol_counts.shape[0]), jnp.int32),
+            pltpu.VMEM(tokens.shape, BF16),
+            pltpu.VMEM((width // LANES, LANES), BF16),
+            pltpu.VMEM((width // LANES, LANES), BF16),
             pltpu.VMEM((depth, total), BF16),
             pltpu.VMEM(flat_keys.shape, BF16),
             pltpu.VMEM(flat_values.shape, BF16),
+            pltpu.VMEM((seqs, 2 * head, (page_table.shape[1] + 1) // 2 * flat_keys.shape[1]), BF16),
             pltpu.VMEM((dp, seqs, depth), BF16),
-            pltpu.VMEM((2, chips, seqs, depth), BF16),
+            pltpu.VMEM((dp, seqs, depth), BF16),
             pltpu.VMEM((chunks, 2, chips * seqs, chunk), F32),
             pltpu.VMEM((chunks, chips * seqs, chunk), F32),
             pltpu.VMEM((chunks, chips - 1, seqs, chunk), F32),
@@ -377,17 +450,18 @@
             pltpu.VMEM((dp, seqs, LANES), F32),
             pltpu.VMEM((dp, 1, dp * seqs), F32),
             pltpu.VMEM((1, dp * seqs), F32),
-            dma((5,)),
-            dma((2, chips)),
-            dma((2, chips)),
+            dma((6,)),
+            dma((3,)),
+            dma(()),
+            dma(()),
+            dma(()),
             dma((chunks,)),
+            dma(()),
             dma((chunks,)),
-            dma((chunks, chips - 1)),
-            dma((chunks, chips - 1)),
-            dma((tp,)),
-            dma((tp,)),
-            dma((dp,)),
-            dma((dp,)),
+            dma(()),
+            dma(()),
+            dma(()),
+            dma(()),
         ],
         compiler_params=pltpu.CompilerParams(
             collective_id=0, has_side_effects=True, vmem_limit_bytes=60 * 1024 * 1024

time: 32.7 us -> 24.3 us (0.74)
  Pallas kernels: 28.6 us -> 21.7 us
  local copies, waits for them, and re-layouts: 1.47 us -> 0.63 us
  between operations: 2.39 us -> 1.8 us
    pallas_call x1, Pallas kernels: 28.6 us -> 21.7 us  [body(): pl.pallas_call(functools.partial(step_kernel, dp, tp), out_shape=(pltpu.V...]
    unnamed x1, local copies, waits for them, and re-layouts: 1.47 us -> 0.63 us
where the time goes in v1:
time: 24.3 us; the launch traced here: 24.1 us
  Pallas kernels  21.7 us (89%)
  between operations  1.8 us (7%)
  local copies, waits for them, and re-layouts  0.63 us (3%)
    pallas_call x1, Pallas kernels, body(): pl.pallas_call(functools.partial(step_kernel, dp, tp), out_shape=(pltpu.V...  21.7 us
    unnamed x1, local copies, waits for them, and re-layouts  0.63 us

profile of v1, /device:TPU:0, one launch (start us, length us, event | category | flops | bytes accessed | tf_op | source)
XLA Modules:
  0.0 24.1 jit_solution(15158261504102285857)
XLA Ops:
  0.6 21.7 %shard_map.122 = (bf16[16,2048]{1,0:T(8,128)(2,1)S(1)}, f32[1,1]{1,0:T(1,128)S(1)}) custom-call(s32[16,32]{1,0:T(8,128)} %table_hbm.1, s32[16]{0:T(128)} %lengths_hbm.1, s32[1,128]{1,0:T(1,128)} %bitcast.10, bf16[16,8192]{1,0:T(8,128)(2,1)} %tokens_hbm.1, bf16[64,128]{1,0:T(8,128)(2,1)} %bitcast.8, bf16[64,128]{1,0:T(8,128)(2,1)} %bitcast.9, ...), custom_call_target="tpu_custom_call" | custom-call | tf_op jit(solution)/shard_map/pallas_call | solution.py:420
  22.4 0.6 %copy.15 = bf16[16,2048]{1,0:T(8,128)(2,1)} copy(bf16[16,2048]{1,0:T(8,128)(2,1)S(1)} %get-tuple-element.6) | data formatting | bytes 131072

commit v2 on v1

--- a/solution.py
+++ b/solution.py
@@ -16,6 +16,9 @@
 BF16 = jnp.bfloat16
 UNROLL = 4
 LANES = 128
+LEVELS = 32000.0
+TINY = 1e-30
+SPLIT = 3
 
 
 def step_kernel(
@@ -44,11 +47,15 @@
     keys,
     values,
     key_columns,
+    weight_sums,
     outgoing,
     spread,
     parts,
     from_pair,
+    outbound,
     from_chips,
+    steps_out,
+    steps_in,
     queries,
     new_keys,
     new_values,
@@ -66,12 +73,15 @@
     pair_recv,
     chip_send,
     chip_recv,
+    step_send,
+    step_recv,
     sum_send,
     sum_recv,
     exc_send,
     exc_recv,
 ):
     chips = dp // 2
+    spread_lanes = steps_out.shape[2]
     me = lax.axis_index("dp")
     zed = lax.axis_index("tensor")
     chip, core = me // 2, me % 2
@@ -86,6 +96,9 @@
     pages = table_ref.shape[1]
     page_rows = keys_hbm.shape[1]
 
+    def wait_bytes(ref, sem):
+        pltpu.make_async_copy(ref, ref, sem).wait()
+
     def partner(dc):
         other, bit = chip, 1
         while bit <= dc:
@@ -107,28 +120,29 @@
                 (tokens_hbm, tokens_ref),
                 (gain_hbm, gain_ref),
                 (lengths_hbm, lengths_ref),
-                (check_hbm, check_ref),
                 (table_hbm, table_ref),
                 (counts_hbm, counts_ref),
+                (check_hbm, check_ref),
             ]
         )
     ]
     for load in small_loads:
         load.start()
     loads = [
+        pltpu.make_async_copy(keys_hbm, keys, load_sems.at[1]),
         pltpu.make_async_copy(wq_hbm, weights.at[:, pl.ds(0, q_width)], load_sems.at[0]),
         pltpu.make_async_copy(wk_hbm, weights.at[:, pl.ds(q_width, kv_width)], load_sems.at[0]),
         pltpu.make_async_copy(
             wv_hbm, weights.at[:, pl.ds(q_width + kv_width, kv_width)], load_sems.at[0]
         ),
-        pltpu.make_async_copy(keys_hbm, keys, load_sems.at[1]),
         pltpu.make_async_copy(values_hbm, values, load_sems.at[2]),
     ]
-    for load in loads:
-        load.start()
-
+
+    loads[0].start()
     for load in small_loads[:2]:
         load.wait()
+    for load in loads[1:4]:
+        load.start()
     square = jnp.zeros((seqs, LANES), F32)
     for j in range(width // LANES):
         part = tokens_ref[:, j * LANES : (j + 1) * LANES].astype(F32)
@@ -170,15 +184,8 @@
     for k in range(1, tp):
         greet_plane(-k)
 
-    for load in small_loads[2:]:
+    for load in small_loads[2:5]:
         load.wait()
-    checks = check_ref[...].astype(F32)
-    checked = jnp.zeros((seqs, LANES), F32)
-    for j in range(width // LANES):
-        at = j * LANES % depth
-        part = outgoing[j * LANES // depth, :, at : at + LANES].astype(F32)
-        checked = checked + part * checks[j : j + 1]
-
     seq_row = lax.broadcasted_iota(jnp.int32, (seqs, LANES), 0)
     positions = jnp.zeros((seqs, LANES), F32)
     for s in range(seqs):
@@ -205,13 +212,33 @@
         key_columns[s] = jnp.transpose(side_by_side(keys, s))
         return carry
 
-    loads[3].wait()
+    loads[0].wait()
+    loads[4].start()
     lax.fori_loop(0, seqs, turn_keys, 0, unroll=UNROLL)
 
-    def wait_bytes(ref, sem):
-        pltpu.make_async_copy(ref, ref, sem).wait()
+    small_loads[5].wait()
+    checks = check_ref[...].astype(F32)
+    checked = jnp.zeros((seqs, LANES), F32)
+    for j in range(width // LANES):
+        at = j * LANES % depth
+        part = outgoing[j * LANES // depth, :, at : at + LANES].astype(F32)
+        checked = checked + part * checks[j : j + 1]
 
     wait_bytes(weights, load_sems.at[0])
+
+    def sum_weights(i, carry):
+        rows = pl.ds(i * 2 * LANES, 2 * LANES)
+        part = weights[rows, pl.ds(0, LANES)].astype(F32)
+        for j in range(1, total // LANES):
+            part = part + weights[rows, pl.ds(j * LANES, LANES)].astype(F32)
+        for term in range(SPLIT):
+            rounded = part.astype(BF16)
+            weight_sums[rows, pl.ds(term * LANES, LANES)] = rounded
+            part = part - rounded.astype(F32)
+        return carry
+
+    lax.fori_loop(0, depth // (2 * LANES), sum_weights, 0)
+
     wait_bytes(spread.at[pl.ds(1, dp - 1)], a2a_recv)
 
     pair_copies = []
@@ -235,22 +262,35 @@
         copy.start()
         pair_copies.append(copy)
         parts[c, 0] = product[:half]
-        return sum(product[:, i : i + LANES] for i in range(0, chunk, LANES))
+
+    spots = lax.broadcasted_iota(jnp.int32, (half - seqs, spread_lanes), 1)
+    spot_rows = lax.broadcasted_iota(jnp.int32, (half - seqs, spread_lanes), 0)
 
     def pass_on(c):
         pair_copies[c].wait_recv()
+        summed = parts[c, 0, pl.ds(seqs, half - seqs)] + from_pair[c, pl.ds(seqs, half - seqs)]
+        largest = jnp.max(jnp.abs(summed), axis=1, keepdims=True)
+        step = (jnp.maximum(largest, TINY) * (1.0 / LEVELS)).astype(BF16).astype(F32)
+        coded = jnp.round(summed * (1.0 / step)).astype(jnp.int32).astype(jnp.int16)
+        for dc in range(1, chips):
+            rows = slice((dc - 1) * seqs, dc * seqs)
+            outbound[c, dc - 1] = coded[rows]
+        steps_out[c] = jnp.sum(jnp.where(spots == spot_rows, step, 0.0), axis=0, keepdims=True)
         for dc in range(chips - 1, 0, -1):
-            rows = pl.ds(dc * seqs, seqs)
-            parts[c, 0, rows] = parts[c, 0, rows] + from_pair[c, rows]
-            copy = pltpu.make_async_remote_copy(
-                src_ref=parts.at[c, 0, rows],
-                dst_ref=from_chips.at[c, dc - 1],
-                send_sem=chip_send,
-                recv_sem=chip_recv.at[c],
-                device_id=(partner(dc) * 2 + core, zed),
-                device_id_type=MESH,
+            send_on(steps_out.at[c], steps_in.at[c, dc - 1], step_send, step_recv.at[c], dc)
+            send_on(
+                outbound.at[c, dc - 1], from_chips.at[c, dc - 1], chip_send, chip_recv.at[c], dc
             )
-            copy.start()
+
+    def send_on(source, target, send_sem, recv_sem, dc):
+        pltpu.make_async_remote_copy(
+            src_ref=source,
+            dst_ref=target,
+            send_sem=send_sem,
+            recv_sem=recv_sem,
+            device_id=(partner(dc) * 2 + core, zed),
+            device_id_type=MESH,
+        ).start()
 
     def exchange(own, everyone, place, targets, send_sem, recv_sem):
         everyone[place] = own[...]
@@ -264,29 +304,32 @@
                 device_id_type=MESH,
             ).start()
 
-    row_sum = jnp.zeros((dp * seqs, LANES), F32)
-    passed = 0
-    for c in range(chunks):
-        row_sum = row_sum + project(c)
-        if c >= 3:
-            pass_on(passed)
-            passed += 1
-    for q in range(2):
-        for dc in range(chips):
-            owner = partner(dc) * 2 + (core + q) % 2
-            at = (q * chips + dc) * seqs
-            share = row_sum[at : at + seqs]
-            if q == 0 and dc == 0:
-                share = share - jnp.where(zed == 0, checked, 0.0)
-            shares[owner] = share
-    turned_sums = jnp.transpose(shares[...].reshape(dp * seqs, LANES))
-    excess_own[...] = jnp.sum(turned_sums, axis=0, keepdims=True)
-    exchange(
-        excess_own, excess_all, me, [((me + k) % dp, zed) for k in range(1, dp)], exc_send, exc_recv
-    )
-    while passed < chunks:
-        pass_on(passed)
-        passed += 1
+    def send_sums():
+        sum_terms = jnp.dot(
+            spread[...].reshape(dp * seqs, depth), weight_sums[...], preferred_element_type=F32
+        )
+        row_sum = sum(sum_terms[:, i * LANES : (i + 1) * LANES] for i in range(SPLIT))
+        for q in range(2):
+            for dc in range(chips):
+                owner = partner(dc) * 2 + (core + q) % 2
+                at = (q * chips + dc) * seqs
+                share = row_sum[at : at + seqs]
+                if q == 0 and dc == 0:
+                    share = share - jnp.where(zed == 0, checked, 0.0)
+                shares[owner] = share
+        turned_sums = jnp.transpose(shares[...].reshape(dp * seqs, LANES))
+        excess_own[...] = jnp.sum(turned_sums, axis=0, keepdims=True)
+        exchange(
+            excess_own, excess_all, me, [((me + k) % dp, zed) for k in range(1, dp)], exc_send, exc_recv
+        )
+
+    for c in range(chunks + 3):
+        if c < chunks:
+            project(c)
+        if c == 1:
+            send_sums()
+        if c >= 2 and c - 2 < chunks:
+            pass_on(c - 2)
     wait_bytes(excess_all.at[pl.ds(1, dp - 1)], exc_recv)
     group_sum = excess_all[0]
     for k in range(1, dp):
@@ -301,6 +344,7 @@
         sums_own, sums_all, zed, [(me, (zed + k) % tp) for k in range(1, tp)], sum_send, sum_recv
     )
 
+
     def rotate(vector):
         return (
             (vector * cosine + pltpu.roll(vector, head // 2, 1) * sine)
@@ -309,10 +353,15 @@
         )
 
     for c in range(chunks):
+        wait_bytes(steps_in.at[c], step_recv.at[c])
         wait_bytes(from_chips.at[c], chip_recv.at[c])
         own = parts[c, 0, pl.ds(0, seqs)] + from_pair[c, pl.ds(0, seqs)]
         for dc in range(1, chips):
-            own = own + from_chips[c, dc - 1]
+            spot = spot_rows[:seqs] + (dc - 1) * seqs
+            step = jnp.sum(
+                jnp.where(spots[:seqs] == spot, steps_in[c, dc - 1], 0.0), axis=1, keepdims=True
+            )
+            own = own + from_chips[c, dc - 1].astype(jnp.int32).astype(F32) * step
         for i in range(chunk // head):
             block = own[:, i * head : (i + 1) * head]
             index = c * (chunk // head) + i
@@ -383,6 +432,7 @@
     wait_bytes(spread.at[pl.ds(1, dp - 1)], a2a_send)
     wait_bytes(from_pair, pair_send)
     wait_bytes(from_chips, chip_send)
+    wait_bytes(steps_in, step_send)
     wait_bytes(sums_all.at[pl.ds(1, tp - 1)], sum_send)
     wait_bytes(excess_all.at[pl.ds(1, dp - 1)], exc_send)
 
@@ -411,6 +461,7 @@
     chips = dp // 2
     chunks = 5 if total % (5 * head) == 0 else 1
     chunk = total // chunks
+    spread_lanes = -(-(chips - 1) * seqs // LANES) * LANES
     flat_keys = key_cache.reshape(key_cache.shape[0], -1, head)
     flat_values = value_cache.reshape(value_cache.shape[0], -1, head)
 
@@ -436,11 +487,15 @@
             pltpu.VMEM(flat_keys.shape, BF16),
             pltpu.VMEM(flat_values.shape, BF16),
             pltpu.VMEM((seqs, 2 * head, (page_table.shape[1] + 1) // 2 * flat_keys.shape[1]), BF16),
+            pltpu.VMEM((depth, SPLIT * LANES), BF16),
             pltpu.VMEM((dp, seqs, depth), BF16),
             pltpu.VMEM((dp, seqs, depth), BF16),
             pltpu.VMEM((chunks, 2, chips * seqs, chunk), F32),
             pltpu.VMEM((chunks, chips * seqs, chunk), F32),
-            pltpu.VMEM((chunks, chips - 1, seqs, chunk), F32),
+            pltpu.VMEM((chunks, chips - 1, seqs, chunk), jnp.int16),
+            pltpu.VMEM((chunks, chips - 1, seqs, chunk), jnp.int16),
+            pltpu.VMEM((chunks, 1, spread_lanes), F32),
+            pltpu.VMEM((chunks, chips - 1, 1, spread_lanes), F32),
             pltpu.VMEM((seqs, q_heads, head), F32),
             pltpu.VMEM((seqs, q_heads, head), F32),
             pltpu.VMEM((seqs, q_heads, head), F32),
@@ -454,6 +509,8 @@
             dma((3,)),
             dma(()),
             dma(()),
+            dma(()),
+            dma((chunks,)),
             dma(()),
             dma((chunks,)),
             dma(()),

time: 24.3 us -> 21.1 us (0.87)
  Pallas kernels: 21.7 us -> 18.5 us
    pallas_call x1, Pallas kernels: 21.7 us -> 18.5 us  [body(): pl.pallas_call(functools.partial(step_kernel, dp, tp), out_shape=(pltpu.V...]
where the time goes in v2:
time: 21.1 us; the launch traced here: 21 us
  Pallas kernels  18.5 us (88%)
  between operations  1.8 us (9%)
  local copies, waits for them, and re-layouts  0.63 us (3%)
    pallas_call x1, Pallas kernels, body(): pl.pallas_call(functools.partial(step_kernel, dp, tp), out_shape=(pltpu.V...  18.5 us
    unnamed x1, local copies, waits for them, and re-layouts  0.63 us

profile of v2, /device:TPU:0, one launch (start us, length us, event | category | flops | bytes accessed | tf_op | source)
XLA Modules:
  0.0 21.0 jit_solution(13460675497753889864)
XLA Ops:
  0.6 18.5 %shard_map.122 = (bf16[16,2048]{1,0:T(8,128)(2,1)S(1)}, f32[1,1]{1,0:T(1,128)S(1)}) custom-call(s32[16,32]{1,0:T(8,128)} %table_hbm.1, s32[16]{0:T(128)} %lengths_hbm.1, s32[1,128]{1,0:T(1,128)} %bitcast.10, bf16[16,8192]{1,0:T(8,128)(2,1)} %tokens_hbm.1, bf16[64,128]{1,0:T(8,128)(2,1)} %bitcast.8, bf16[64,128]{1,0:T(8,128)(2,1)} %bitcast.9, ...), custom_call_target="tpu_custom_call" | custom-call | tf_op jit(solution)/shard_map/pallas_call | solution.py:471
  19.2 0.6 %copy.15 = bf16[16,2048]{1,0:T(8,128)(2,1)} copy(bf16[16,2048]{1,0:T(8,128)(2,1)S(1)} %get-tuple-element.6) | data formatting | bytes 131072

commit v3 on v2

--- a/solution.py
+++ b/solution.py
@@ -48,6 +48,7 @@
     values,
     key_columns,
     weight_sums,
+    check_row,
     outgoing,
     spread,
     parts,
@@ -107,6 +108,9 @@
             bit *= 2
         return other
 
+    def slot(q, dc):
+        return (1 - q if dc else q) * chips + dc
+
     barrier = pltpu.get_barrier_semaphore()
     for k in range(1, dp):
         pl.semaphore_signal(
@@ -166,13 +170,12 @@
 
 
     for dc in range(chips - 1, -1, -1):
-        for q in range(2):
-            if dc == 0 and q == 0:
-                continue
-            target = partner(dc) * 2 + (core + q) % 2
+        for there in range(2) if dc else [1 - core]:
+            q = (there + core) % 2
+            target = partner(dc) * 2 + there
             copy = pltpu.make_async_remote_copy(
                 src_ref=outgoing.at[target],
-                dst_ref=spread.at[q * chips + dc],
+                dst_ref=spread.at[slot(q, dc)],
                 send_sem=a2a_send,
                 recv_sem=a2a_recv,
                 device_id=(target, zed),
@@ -223,25 +226,31 @@
         at = j * LANES % depth
         part = outgoing[j * LANES // depth, :, at : at + LANES].astype(F32)
         checked = checked + part * checks[j : j + 1]
+    shares[...] = jnp.zeros(shares.shape, F32)
+    shares[me] = jnp.where(zed == 0, checked, 0.0)
+    turned_checks = jnp.transpose(shares[...].reshape(dp * seqs, LANES))
+    check_row[...] = jnp.sum(turned_checks, axis=0, keepdims=True)
 
     wait_bytes(weights, load_sems.at[0])
 
-    def sum_weights(i, carry):
-        rows = pl.ds(i * 2 * LANES, 2 * LANES)
-        part = weights[rows, pl.ds(0, LANES)].astype(F32)
-        for j in range(1, total // LANES):
-            part = part + weights[rows, pl.ds(j * LANES, LANES)].astype(F32)
-        for term in range(SPLIT):
-            rounded = part.astype(BF16)
-            weight_sums[rows, pl.ds(term * LANES, LANES)] = rounded
-            part = part - rounded.astype(F32)
-        return carry
-
-    lax.fori_loop(0, depth // (2 * LANES), sum_weights, 0)
+    totals = lax.dot_general(
+        jnp.ones((seqs, total), BF16),
+        weights[...],
+        (((1,), (1,)), ((), ())),
+        preferred_element_type=F32,
+    )
+    term = lax.broadcasted_iota(jnp.int32, (seqs, depth), 0)
+    split = jnp.zeros((seqs, depth), F32)
+    for i in range(SPLIT):
+        rounded = totals.astype(BF16).astype(F32)
+        split = jnp.where(term == i, rounded, split)
+        totals = totals - rounded
+    weight_sums[...] = split.astype(BF16)
 
     wait_bytes(spread.at[pl.ds(1, dp - 1)], a2a_recv)
 
     pair_copies = []
+    batch = seqs // 2
     half = chips * seqs
 
     def project(c):
@@ -271,15 +280,28 @@
         summed = parts[c, 0, pl.ds(seqs, half - seqs)] + from_pair[c, pl.ds(seqs, half - seqs)]
         largest = jnp.max(jnp.abs(summed), axis=1, keepdims=True)
         step = (jnp.maximum(largest, TINY) * (1.0 / LEVELS)).astype(BF16).astype(F32)
-        coded = jnp.round(summed * (1.0 / step)).astype(jnp.int32).astype(jnp.int16)
+        coded = jnp.round(summed * (1.0 / step)).astype(jnp.int32)
         for dc in range(1, chips):
-            rows = slice((dc - 1) * seqs, dc * seqs)
-            outbound[c, dc - 1] = coded[rows]
+            for h in range(2):
+                at = (dc - 1) * seqs + h * batch
+                stacked = jnp.concatenate(
+                    [coded[at : at + batch, : chunk // 2], coded[at : at + batch, chunk // 2 :]],
+                    axis=0,
+                )
+                outbound[h, c, dc - 1] = stacked.astype(jnp.int16)
         steps_out[c] = jnp.sum(jnp.where(spots == spot_rows, step, 0.0), axis=0, keepdims=True)
         for dc in range(chips - 1, 0, -1):
             send_on(steps_out.at[c], steps_in.at[c, dc - 1], step_send, step_recv.at[c], dc)
+        send_batch(0, c)
+
+    def send_batch(h, c):
+        for dc in range(chips - 1, 0, -1):
             send_on(
-                outbound.at[c, dc - 1], from_chips.at[c, dc - 1], chip_send, chip_recv.at[c], dc
+                outbound.at[h, c, dc - 1],
+                from_chips.at[h, c, dc - 1],
+                chip_send,
+                chip_recv.at[c if h == 0 else chunks],
+                dc,
             )
 
     def send_on(source, target, send_sem, recv_sem, dc):
@@ -288,7 +310,7 @@
             dst_ref=target,
             send_sem=send_sem,
             recv_sem=recv_sem,
-            device_id=(partner(dc) * 2 + core, zed),
+            device_id=(partner(dc) * 2 + (core + 1) % 2, zed),
             device_id_type=MESH,
         ).start()
 
@@ -305,78 +327,88 @@
             ).start()
 
     def send_sums():
-        sum_terms = jnp.dot(
-            spread[...].reshape(dp * seqs, depth), weight_sums[...], preferred_element_type=F32
-        )
-        row_sum = sum(sum_terms[:, i * LANES : (i + 1) * LANES] for i in range(SPLIT))
-        for q in range(2):
-            for dc in range(chips):
-                owner = partner(dc) * 2 + (core + q) % 2
-                at = (q * chips + dc) * seqs
-                share = row_sum[at : at + seqs]
-                if q == 0 and dc == 0:
-                    share = share - jnp.where(zed == 0, checked, 0.0)
-                shares[owner] = share
-        turned_sums = jnp.transpose(shares[...].reshape(dp * seqs, LANES))
-        excess_own[...] = jnp.sum(turned_sums, axis=0, keepdims=True)
+        blocks = []
+        for owner in range(dp):
+            there = owner // 2
+            relative, bit = 0, 1
+            while bit < chips:
+                mine, other = chip // bit % 2, there // bit % 2
+                relative = relative + bit * ((mine + other) % 2)
+                bit *= 2
+            kept = (core + owner + (relative + chips - 1) // chips) % 2
+            blocks.append(spread[kept * chips + relative])
+        terms = lax.dot_general(
+            weight_sums[...],
+            jnp.concatenate(blocks, axis=0),
+            (((1,), (1,)), ((), ())),
+            preferred_element_type=F32,
+        )
+        excess_own[...] = jnp.sum(terms, axis=0, keepdims=True) - check_row[...]
         exchange(
             excess_own, excess_all, me, [((me + k) % dp, zed) for k in range(1, dp)], exc_send, exc_recv
         )
 
-    for c in range(chunks + 3):
-        if c < chunks:
-            project(c)
-        if c == 1:
+    for c in range(chunks):
+        project(c)
+        if c == 0:
             send_sums()
-        if c >= 2 and c - 2 < chunks:
-            pass_on(c - 2)
-    wait_bytes(excess_all.at[pl.ds(1, dp - 1)], exc_recv)
-    group_sum = excess_all[0]
-    for k in range(1, dp):
-        group_sum = group_sum + excess_all[k]
-    sums_own[...] = group_sum
-
-    @pl.when(zed < tp - 1)
-    def _():
-        pl.semaphore_wait(barrier, tp - 1 - zed)
-
-    exchange(
-        sums_own, sums_all, zed, [(me, (zed + k) % tp) for k in range(1, tp)], sum_send, sum_recv
-    )
-
-
-    def rotate(vector):
+        if c >= 3:
+            pass_on(c - 3)
+    for c in range(max(chunks - 3, 0), chunks):
+        pass_on(c)
+    for c in range(chunks):
+        send_batch(1, c)
+
+    def finish_group():
+        wait_bytes(excess_all.at[pl.ds(1, dp - 1)], exc_recv)
+        group_sum = excess_all[0]
+        for k in range(1, dp):
+            group_sum = group_sum + excess_all[k]
+        sums_own[...] = group_sum
+
+        @pl.when(zed < tp - 1)
+        def _():
+            pl.semaphore_wait(barrier, tp - 1 - zed)
+
+        exchange(
+            sums_own, sums_all, zed, [(me, (zed + k) % tp) for k in range(1, tp)], sum_send, sum_recv
+        )
+
+    def rotate(vector, rows):
         return (
-            (vector * cosine + pltpu.roll(vector, head // 2, 1) * sine)
+            (vector * cosine[rows] + pltpu.roll(vector, head // 2, 1) * sine[rows])
             .astype(BF16)
             .astype(F32)
         )
 
-    for c in range(chunks):
-        wait_bytes(steps_in.at[c], step_recv.at[c])
-        wait_bytes(from_chips.at[c], chip_recv.at[c])
-        own = parts[c, 0, pl.ds(0, seqs)] + from_pair[c, pl.ds(0, seqs)]
+    def settle(h, c):
+        if h == 0:
+            wait_bytes(steps_in.at[c], step_recv.at[c])
+            wait_bytes(from_chips.at[h, c], chip_recv.at[c])
+        rows = slice(h * batch, (h + 1) * batch)
+        own = parts[c, 0, rows] + from_pair[c, rows]
         for dc in range(1, chips):
-            spot = spot_rows[:seqs] + (dc - 1) * seqs
+            spot = spot_rows[rows] + (dc - 1) * seqs
             step = jnp.sum(
-                jnp.where(spots[:seqs] == spot, steps_in[c, dc - 1], 0.0), axis=1, keepdims=True
+                jnp.where(spots[rows] == spot, steps_in[c, dc - 1], 0.0), axis=1, keepdims=True
             )
-            own = own + from_chips[c, dc - 1].astype(jnp.int32).astype(F32) * step
+            stacked = from_chips[h, c, dc - 1].astype(jnp.int32).astype(F32)
+            own = own + jnp.concatenate([stacked[:batch], stacked[batch:]], axis=1) * step
         for i in range(chunk // head):
             block = own[:, i * head : (i + 1) * head]
             index = c * (chunk // head) + i
             if index < q_heads:
-                queries[:, index, :] = rotate(block)
+                queries[rows, index, :] = rotate(block, rows)
             elif index < q_heads + kv_heads:
                 k = index - q_heads
-                turned = rotate(block)
+                turned = rotate(block, rows)
                 for g in range(group):
-                    new_keys[:, k * group + g, :] = turned
+                    new_keys[rows, k * group + g, :] = turned
             else:
                 k = index - q_heads - kv_heads
                 rounded = block.astype(BF16).astype(F32)
                 for g in range(group):
-                    new_values[:, k * group + g, :] = rounded
+                    new_values[rows, k * group + g, :] = rounded
 
     column = lax.broadcasted_iota(jnp.int32, (2 * q_heads, span), 1)
     row = lax.broadcasted_iota(jnp.int32, (2 * q_heads, span), 0)
@@ -415,8 +447,15 @@
         result = result + new_weight.astype(BF16).astype(F32) * new_values[s]
         mixed[s] = result / denominator
 
-    for s in range(seqs):
-        one_sequence(s)
+    for h in range(2):
+        if h == 0:
+            finish_group()
+        else:
+            wait_bytes(from_chips.at[1], chip_recv.at[chunks])
+        for c in range(chunks):
+            settle(h, c)
+        for s in range(h * batch, (h + 1) * batch):
+            one_sequence(s)
 
     for h in range(q_heads):
         out_ref[:, h * head : (h + 1) * head] = mixed[:, h, :].astype(BF16)
@@ -487,13 +526,14 @@
             pltpu.VMEM(flat_keys.shape, BF16),
             pltpu.VMEM(flat_values.shape, BF16),
             pltpu.VMEM((seqs, 2 * head, (page_table.shape[1] + 1) // 2 * flat_keys.shape[1]), BF16),
-            pltpu.VMEM((depth, SPLIT * LANES), BF16),
+            pltpu.VMEM((seqs, depth), BF16),
+            pltpu.VMEM((1, dp * seqs), F32),
             pltpu.VMEM((dp, seqs, depth), BF16),
             pltpu.VMEM((dp, seqs, depth), BF16),
             pltpu.VMEM((chunks, 2, chips * seqs, chunk), F32),
             pltpu.VMEM((chunks, chips * seqs, chunk), F32),
-            pltpu.VMEM((chunks, chips - 1, seqs, chunk), jnp.int16),
-            pltpu.VMEM((chunks, chips - 1, seqs, chunk), jnp.int16),
+            pltpu.VMEM((2, chunks, chips - 1, seqs, chunk // 2), jnp.int16),
+            pltpu.VMEM((2, chunks, chips - 1, seqs, chunk // 2), jnp.int16),
             pltpu.VMEM((chunks, 1, spread_lanes), F32),
             pltpu.VMEM((chunks, chips - 1, 1, spread_lanes), F32),
             pltpu.VMEM((seqs, q_heads, head), F32),
@@ -512,7 +552,7 @@
             dma(()),
             dma((chunks,)),
             dma(()),
-            dma((chunks,)),
+            dma((chunks + 1,)),
             dma(()),
             dma((chunks,)),
             dma(()),

time: 21.1 us -> 20.4 us (0.967)
  Pallas kernels: 18.5 us -> 17.9 us
    pallas_call x1, Pallas kernels: 18.5 us -> 17.9 us  [body(): pl.pallas_call(functools.partial(step_kernel, dp, tp), out_shape=(pltpu.V...]
where the time goes in v3:
time: 20.4 us; the launch traced here: 20.3 us
  Pallas kernels  17.9 us (88%)
  between operations  1.8 us (9%)
  local copies, waits for them, and re-layouts  0.63 us (3%)
    pallas_call x1, Pallas kernels, body(): pl.pallas_call(functools.partial(step_kernel, dp, tp), out_shape=(pltpu.V...  17.9 us
    unnamed x1, local copies, waits for them, and re-layouts  0.63 us

profile of v3, /device:TPU:0, one launch (start us, length us, event | category | flops | bytes accessed | tf_op | source)
XLA Modules:
  0.0 20.3 jit_solution(8268301184458652286)
XLA Ops:
  0.6 17.9 %shard_map.122 = (bf16[16,2048]{1,0:T(8,128)(2,1)S(1)}, f32[1,1]{1,0:T(1,128)S(1)}) custom-call(s32[16,32]{1,0:T(8,128)} %table_hbm.1, s32[16]{0:T(128)} %lengths_hbm.1, s32[1,128]{1,0:T(1,128)} %bitcast.10, bf16[16,8192]{1,0:T(8,128)(2,1)} %tokens_hbm.1, bf16[64,128]{1,0:T(8,128)(2,1)} %bitcast.8, bf16[64,128]{1,0:T(8,128)(2,1)} %bitcast.9, ...), custom_call_target="tpu_custom_call" | custom-call | tf_op jit(solution)/shard_map/pallas_call | solution.py:510
  18.5 0.6 %copy.15 = bf16[16,2048]{1,0:T(8,128)(2,1)} copy(bf16[16,2048]{1,0:T(8,128)(2,1)S(1)} %get-tuple-element.6) | data formatting | bytes 131072

commit v4 on v3

--- a/solution.py
+++ b/solution.py
@@ -456,9 +456,9 @@
             settle(h, c)
         for s in range(h * batch, (h + 1) * batch):
             one_sequence(s)
-
-    for h in range(q_heads):
-        out_ref[:, h * head : (h + 1) * head] = mixed[:, h, :].astype(BF16)
+        rows = slice(h * batch, (h + 1) * batch)
+        for i in range(q_heads):
+            out_ref[rows, i * head : (i + 1) * head] = mixed[rows, i, :].astype(BF16)
 
     wait_bytes(sums_all.at[pl.ds(1, tp - 1)], sum_recv)
     grand = sums_all[0]
@@ -466,7 +466,9 @@
         grand = grand + sums_all[k]
     residual = grand / math.sqrt(total * tp)
     over = jnp.maximum(jnp.abs(residual) - TOL_STEP * counts_ref[...].astype(F32), 0.0)
-    excess_ref[...] = jnp.sum(over, axis=1, keepdims=True) / math.sqrt(seqs * dp)
+    excess_ref[...] = jnp.broadcast_to(
+        jnp.sum(over, axis=1, keepdims=True) / math.sqrt(seqs * dp), excess_ref.shape
+    )
 
     wait_bytes(spread.at[pl.ds(1, dp - 1)], a2a_send)
     wait_bytes(from_pair, pair_send)
@@ -474,6 +476,16 @@
     wait_bytes(steps_in, step_send)
     wait_bytes(sums_all.at[pl.ds(1, tp - 1)], sum_send)
     wait_bytes(excess_all.at[pl.ds(1, dp - 1)], exc_send)
+
+
+def hand_out(attention, excess, attention_out, excess_out, single, sems):
+    first = pltpu.make_async_copy(attention, attention_out, sems.at[0])
+    first.start()
+    single[...] = excess[0:1, 0:1]
+    second = pltpu.make_async_copy(single, excess_out, sems.at[1])
+    second.start()
+    first.wait()
+    second.wait()
 
 
 def body(
@@ -511,7 +523,7 @@
         functools.partial(step_kernel, dp, tp),
         out_shape=(
             pltpu.VMEM((seqs, q_width), BF16),
-            pltpu.VMEM((1, 1), F32),
+            pltpu.VMEM((8, LANES), F32),
         ),
         in_specs=[hbm] * 11,
         out_specs=(vmem, vmem),
@@ -576,6 +588,19 @@
         flat_keys,
         flat_values,
     )
+    attention, excess = pl.pallas_call(
+        hand_out,
+        out_shape=(
+            jax.ShapeDtypeStruct((seqs, q_width), BF16),
+            jax.ShapeDtypeStruct((1, 1), F32),
+        ),
+        in_specs=[vmem, vmem],
+        out_specs=(hbm, hbm),
+        scratch_shapes=[pltpu.VMEM((1, 1), F32), dma((2,))],
+    )(
+        pltpu.with_memory_space_constraint(attention, pltpu.VMEM),
+        pltpu.with_memory_space_constraint(excess, pltpu.VMEM),
+    )
     return attention, excess[0, 0]
 
 

time: 20.4 us -> 19.3 us (0.946)
  between operations: 1.8 us -> 0.64 us
  local copies, waits for them, and re-layouts: 0.63 us -> 0 us
  Pallas kernels: 17.9 us -> 18.5 us
    pallas_call x0 -> x1, Pallas kernels: none -> 0.65 us  [body(): pl.pallas_call(hand_out, out_shape=(jax.ShapeDtypeStruct((seqs, q_width),...]
    unnamed x1 -> x0, local copies, waits for them, and re-layouts: 0.63 us -> none
where the time goes in v4:
time: 19.3 us; the launch traced here: 19.2 us
  Pallas kernels  18.5 us (96%)
  between operations  0.64 us (3%)
    pallas_call x1, Pallas kernels, body(): pl.pallas_call(functools.partial(step_kernel, dp, tp), out_shape=(pltpu.V...  17.9 us
    pallas_call x1, Pallas kernels, body(): pl.pallas_call(hand_out, out_shape=(jax.ShapeDtypeStruct((seqs, q_width),...  0.65 us

profile of v4, /device:TPU:0, one launch (start us, length us, event | category | flops | bytes accessed | tf_op | source)
XLA Modules:
  0.0 19.2 jit_solution(1673637199859090313)
XLA Ops:
  0.6 17.9 %shard_map.122 = (bf16[16,2048]{1,0:T(8,128)(2,1)S(1)}, f32[8,128]{1,0:T(8,128)S(1)}) custom-call(s32[16,32]{1,0:T(8,128)} %table_hbm.1, s32[16]{0:T(128)} %lengths_hbm.1, s32[1,128]{1,0:T(1,128)} %bitcast.10, bf16[16,8192]{1,0:T(8,128)(2,1)} %tokens_hbm.1, bf16[64,128]{1,0:T(8,128)(2,1)} %bitcast.8, bf16[64,128]{1,0:T(8,128)(2,1)} %bitcast.9, ...), custom_call_target="tpu_custom_call" | custom-call | tf_op jit(solution)/shard_map/pallas_call | solution.py:522
  18.5 0.7 %shard_map.123 = (bf16[16,2048]{1,0:T(8,128)(2,1)}, f32[1,1]{1,0:T(1,128)}) custom-call(bf16[16,2048]{1,0:T(8,128)(2,1)S(1)} %get-tuple-element.6.attention, f32[8,128]{1,0:T(8,128)S(1)} %get-tuple-element.7.excess), custom_call_target="tpu_custom_call" | custom-call | tf_op jit(solution)/shard_map/pallas_call | solution.py:591

commit v5 on v4

--- a/solution.py
+++ b/solution.py
@@ -250,6 +250,8 @@
     wait_bytes(spread.at[pl.ds(1, dp - 1)], a2a_recv)
 
     pair_copies = []
+    middle = (chunks + 1) // 2
+    step_groups = [(0, middle)] + [(middle, chunks)] * (chunks > 1)
     batch = seqs // 2
     half = chips * seqs
 
@@ -290,8 +292,17 @@
                 )
                 outbound[h, c, dc - 1] = stacked.astype(jnp.int16)
         steps_out[c] = jnp.sum(jnp.where(spots == spot_rows, step, 0.0), axis=0, keepdims=True)
-        for dc in range(chips - 1, 0, -1):
-            send_on(steps_out.at[c], steps_in.at[c, dc - 1], step_send, step_recv.at[c], dc)
+        for g, (first, last) in enumerate(step_groups):
+            if c == last - 1:
+                some = pl.ds(first, last - first)
+                for dc in range(chips - 1, 0, -1):
+                    send_on(
+                        steps_out.at[some],
+                        steps_in.at[dc - 1, some],
+                        step_send,
+                        step_recv.at[g],
+                        dc,
+                    )
         send_batch(0, c)
 
     def send_batch(h, c):
@@ -326,7 +337,7 @@
                 device_id_type=MESH,
             ).start()
 
-    def send_sums():
+    def add_sums():
         blocks = []
         for owner in range(dp):
             there = owner // 2
@@ -344,10 +355,13 @@
             preferred_element_type=F32,
         )
         excess_own[...] = jnp.sum(terms, axis=0, keepdims=True) - check_row[...]
+
+    def send_sums():
         exchange(
             excess_own, excess_all, me, [((me + k) % dp, zed) for k in range(1, dp)], exc_send, exc_recv
         )
 
+    add_sums()
     for c in range(chunks):
         project(c)
         if c == 0:
@@ -383,14 +397,17 @@
 
     def settle(h, c):
         if h == 0:
-            wait_bytes(steps_in.at[c], step_recv.at[c])
+            for g, (first, last) in enumerate(step_groups):
+                if c == first:
+                    some = pl.ds(first, last - first)
+                    wait_bytes(steps_in.at[:, some], step_recv.at[g])
             wait_bytes(from_chips.at[h, c], chip_recv.at[c])
         rows = slice(h * batch, (h + 1) * batch)
         own = parts[c, 0, rows] + from_pair[c, rows]
         for dc in range(1, chips):
             spot = spot_rows[rows] + (dc - 1) * seqs
             step = jnp.sum(
-                jnp.where(spots[rows] == spot, steps_in[c, dc - 1], 0.0), axis=1, keepdims=True
+                jnp.where(spots[rows] == spot, steps_in[dc - 1, c], 0.0), axis=1, keepdims=True
             )
             stacked = from_chips[h, c, dc - 1].astype(jnp.int32).astype(F32)
             own = own + jnp.concatenate([stacked[:batch], stacked[batch:]], axis=1) * step
@@ -547,7 +564,7 @@
             pltpu.VMEM((2, chunks, chips - 1, seqs, chunk // 2), jnp.int16),
             pltpu.VMEM((2, chunks, chips - 1, seqs, chunk // 2), jnp.int16),
             pltpu.VMEM((chunks, 1, spread_lanes), F32),
-            pltpu.VMEM((chunks, chips - 1, 1, spread_lanes), F32),
+            pltpu.VMEM((chips - 1, chunks, 1, spread_lanes), F32),
             pltpu.VMEM((seqs, q_heads, head), F32),
             pltpu.VMEM((seqs, q_heads, head), F32),
             pltpu.VMEM((seqs, q_heads, head), F32),
@@ -566,7 +583,7 @@
             dma(()),
             dma((chunks + 1,)),
             dma(()),
-            dma((chunks,)),
+            dma((2,)),
             dma(()),
             dma(()),
             dma(()),

time: 19.3 us -> 19.1 us (0.990)
  Pallas kernels: 18.5 us -> 18.3 us
    pallas_call x1, Pallas kernels: 17.9 us -> 17.6 us  [body(): pl.pallas_call(functools.partial(step_kernel, dp, tp), out_shape=(pltpu.V...]
where the time goes in v5:
time: 19.1 us; the launch traced here: 18.9 us
  Pallas kernels  18.3 us (96%)
  between operations  0.64 us (3%)
    pallas_call x1, Pallas kernels, body(): pl.pallas_call(functools.partial(step_kernel, dp, tp), out_shape=(pltpu.V...  17.6 us
    pallas_call x1, Pallas kernels, body(): pl.pallas_call(hand_out, out_shape=(jax.ShapeDtypeStruct((seqs, q_width),...  0.65 us

profile of v5, /device:TPU:0, one launch (start us, length us, event | category | flops | bytes accessed | tf_op | source)
XLA Modules:
  0.0 18.9 jit_solution(15126359617643709953)
XLA Ops:
  0.6 17.6 %shard_map.122 = (bf16[16,2048]{1,0:T(8,128)(2,1)S(1)}, f32[8,128]{1,0:T(8,128)S(1)}) custom-call(s32[16,32]{1,0:T(8,128)} %table_hbm.1, s32[16]{0:T(128)} %lengths_hbm.1, s32[1,128]{1,0:T(1,128)} %bitcast.10, bf16[16,8192]{1,0:T(8,128)(2,1)} %tokens_hbm.1, bf16[64,128]{1,0:T(8,128)(2,1)} %bitcast.8, bf16[64,128]{1,0:T(8,128)(2,1)} %bitcast.9, ...), custom_call_target="tpu_custom_call" | custom-call | tf_op jit(solution)/shard_map/pallas_call | solution.py:539
  18.3 0.7 %shard_map.123 = (bf16[16,2048]{1,0:T(8,128)(2,1)}, f32[1,1]{1,0:T(1,128)}) custom-call(bf16[16,2048]{1,0:T(8,128)(2,1)S(1)} %get-tuple-element.6.attention, f32[8,128]{1,0:T(8,128)S(1)} %get-tuple-element.7.excess), custom_call_target="tpu_custom_call" | custom-call | tf_op jit(solution)/shard_map/pallas_call | solution.py:608

commit v6 on v5

--- a/solution.py
+++ b/solution.py
@@ -434,7 +434,7 @@
         column // kv_heads + row // q_heads * (span // kv_heads),
         pages * page_rows,
     )
-    score_scale = head ** (-0.5)
+    exponent_scale = head ** (-0.5) * math.log2(math.e)
     no_query = jnp.zeros((q_heads, head), BF16)
     loads[4].wait()
 
@@ -448,13 +448,13 @@
             ],
             axis=0,
         )
-        scores = jnp.dot(paired, key_columns[s], preferred_element_type=F32) * score_scale
-        new_score = jnp.sum(query * new_keys[s], axis=1, keepdims=True) * score_scale
+        scores = jnp.dot(paired, key_columns[s], preferred_element_type=F32)
+        new_score = jnp.sum(query * new_keys[s], axis=1, keepdims=True)
         masked = jnp.where(place < lengths_ref[s], scores, -jnp.inf)
         highest = jnp.max(masked, axis=1, keepdims=True)
         peak = jnp.maximum(jnp.maximum(highest[:q_heads], highest[q_heads:]), new_score)
-        soft = jnp.exp(masked - jnp.concatenate([peak, peak], axis=0))
-        new_weight = jnp.exp(new_score - peak)
+        soft = jnp.exp2((masked - jnp.concatenate([peak, peak], axis=0)) * exponent_scale)
+        new_weight = jnp.exp2((new_score - peak) * exponent_scale)
         sums = jnp.sum(soft, axis=1, keepdims=True)
         denominator = sums[:q_heads] + sums[q_heads:] + new_weight
         result = jnp.dot(

time: 19.1 us -> 19.1 us (level)
  no operation moved by 1% of the time
where the time goes in v6:
time: 19.1 us; the launch traced here: 18.9 us
  Pallas kernels  18.3 us (96%)
  between operations  0.64 us (3%)
    pallas_call x1, Pallas kernels, body(): pl.pallas_call(functools.partial(step_kernel, dp, tp), out_shape=(pltpu.V...  17.6 us
    pallas_call x1, Pallas kernels, body(): pl.pallas_call(hand_out, out_shape=(jax.ShapeDtypeStruct((seqs, q_width),...  0.65 us

profile of v6, /device:TPU:0, one launch (start us, length us, event | category | flops | bytes accessed | tf_op | source)
XLA Modules:
  0.0 18.9 jit_solution(5286547435226012697)
XLA Ops:
  0.6 17.6 %shard_map.122 = (bf16[16,2048]{1,0:T(8,128)(2,1)S(1)}, f32[8,128]{1,0:T(8,128)S(1)}) custom-call(s32[16,32]{1,0:T(8,128)} %table_hbm.1, s32[16]{0:T(128)} %lengths_hbm.1, s32[1,128]{1,0:T(1,128)} %bitcast.10, bf16[16,8192]{1,0:T(8,128)(2,1)} %tokens_hbm.1, bf16[64,128]{1,0:T(8,128)(2,1)} %bitcast.8, bf16[64,128]{1,0:T(8,128)(2,1)} %bitcast.9, ...), custom_call_target="tpu_custom_call" | custom-call | tf_op jit(solution)/shard_map/pallas_call | solution.py:539
  18.3 0.7 %shard_map.123 = (bf16[16,2048]{1,0:T(8,128)(2,1)}, f32[1,1]{1,0:T(1,128)}) custom-call(bf16[16,2048]{1,0:T(8,128)(2,1)S(1)} %get-tuple-element.6.attention, f32[8,128]{1,0:T(8,128)S(1)} %get-tuple-element.7.excess), custom_call_target="tpu_custom_call" | custom-call | tf_op jit(solution)/shard_map/pallas_call | solution.py:608
